TPU v7x, 32 devices: a whole 2x2x4 slice. The times are simulated.
32 devices in a mesh: mem: 8 (over y, x, core), col: 4 (over z).
Axes of the slice: x: 2, y: 2, z: 4, core: 2. Of those that a mesh axis runs over, the one named last changes fastest.
Arguments:
- background_trials: bfloat16 [256, 4, 32, 512], P('mem', None, None, 'col'), may hold values from -6 to 6
- region_active_tally: int32 [8, 16], P('mem', 'col'), may hold values from 256 to 2048, as said below
- sensed_component: int32 [8, 16, 2048], P('mem', 'col'), may hold values from 0 to 1919
- distance_bucket: int32 [8, 16, 2048], P('mem', 'col'), may hold values from 0 to 15
- sensor_readings: float32 [8, 16, 2048], P('mem', 'col'), may hold values from -6 to 6
- inverse_noise_variance: float32 [8, 16, 2048], P('mem', 'col'), may hold values from 0.25 to 4
- localization_factors: float32 [16], replicated, may hold values from 0.05 to 1
Outputs:
- analysis: bfloat16 [256, 4, 32, 512], P('mem', None, None, 'col')
Inputs may be any that keep to these rules, and one draw needn't show every extreme that they name: `region_active_tally`: observations of a patch fill its first slots; some patch has exactly 2048 live observations.
All inputs are finite; a program needn't handle non-finite values.
Results may differ from a plain program's by a relative error of at most 0.0063.
Values may be sent and summed in bfloat16 or wider, within the bound.
No kernel may reach another device: no remote copies, remote signals or barrier semaphores. Data moves between devices by JAX's collectives and lax.ppermute only.
A program may use at most 64 MiB of HBM per device.

v0:
```python
import jax
import jax.numpy as jnp
from jax import lax
from jax.sharding import PartitionSpec as P

SECTOR_SPAN = 32
REACH_MARGIN = 4
ITERS = 4
inflation = 1.1
obs_block = 128


def padded(block, sides, width):
    for axis, dim in sides:
        count = lax.axis_size(axis)
        forward = [(i, i + 1) for i in range(count - 1)]
        backward = [(target, source) for source, target in forward]
        low = lax.ppermute(
            lax.slice_in_dim(block, block.shape[dim] - width, None, axis=dim), axis, forward
        )
        high = lax.ppermute(lax.slice_in_dim(block, 0, width, axis=dim), axis, backward)
        block = jnp.concatenate([low, block, high], axis=dim)
    return block


def lookup(class_ids, weight_table):
    table_slots = jnp.arange(weight_table.shape[0], dtype=jnp.int32)
    return jnp.sum(jnp.where(class_ids[..., None] == table_slots, weight_table, 0.0), axis=-1)


def observe(
    anomaly_flat, average_flat, cell_ids, class_ids, values, inv_var, is_live, weight_table
):
    observed = jnp.take_along_axis(anomaly_flat, cell_ids[:, None, :], axis=2)
    innovation = values - jnp.take_along_axis(average_flat, cell_ids, axis=1)
    weight = jnp.where(is_live, inv_var * lookup(class_ids, weight_table), 0.0)
    scaled = (observed.astype(jnp.float32) * weight[:, None, :]).astype(jnp.bfloat16)
    gram_part = jnp.einsum("qkm,qjm->qkj", scaled, observed, preferred_element_type=jnp.float32)
    forcing_part = jnp.einsum(
        "qkm,qm->qk", scaled.astype(jnp.float32), innovation, precision=lax.Precision.HIGHEST
    )
    return (gram_part, forcing_part)


def local(
    background_trials,
    region_active_tally,
    sensed_component,
    distance_bucket,
    sensor_readings,
    inverse_noise_variance,
    localization_factors,
):
    local_region_tile = lax.all_to_all(
        background_trials, "mem", split_axis=2, concat_axis=0, tiled=True
    )
    enlarged_piece = padded(local_region_tile, (("mem", 2), ("col", 3)), REACH_MARGIN)
    trial_flattened = enlarged_piece.shape[0]
    physical_quantity_stack = enlarged_piece.shape[1]
    tile_height = enlarged_piece.shape[2] - 2 * REACH_MARGIN
    tile_width = enlarged_piece.shape[3] - 2 * REACH_MARGIN
    patches = tile_width // SECTOR_SPAN
    frame_breadth = SECTOR_SPAN + 2 * REACH_MARGIN
    unit_weights = jnp.ones((trial_flattened,), jnp.bfloat16)
    predicted_average = (
        lax.dot_general(
            unit_weights,
            enlarged_piece,
            (((0,), (0,)), ((), ())),
            preferred_element_type=jnp.float32,
        )
        / trial_flattened
    )
    deviation_matrix = (enlarged_piece.astype(jnp.float32) - predicted_average).astype(jnp.bfloat16)
    anomaly_flat = jnp.stack(
        [
            deviation_matrix[
                :, :, :, sector_index * SECTOR_SPAN : sector_index * SECTOR_SPAN + frame_breadth
            ]
            for sector_index in range(patches)
        ]
    ).reshape(patches, trial_flattened, -1)
    average_flat = jnp.stack(
        [
            predicted_average[
                :, :, sector_index * SECTOR_SPAN : sector_index * SECTOR_SPAN + frame_breadth
            ]
            for sector_index in range(patches)
        ]
    ).reshape(patches, -1)
    counts = region_active_tally.reshape(patches)
    cell_ids = sensed_component.reshape(patches, -1)
    class_ids = distance_bucket.reshape(patches, -1)
    values = sensor_readings.reshape(patches, -1)
    inv_vars = inverse_noise_variance.reshape(patches, -1)
    order_ids = jnp.broadcast_to(jnp.arange(cell_ids.shape[1], dtype=jnp.int32), cell_ids.shape)
    rounds = (jnp.max(counts) + obs_block - 1) // obs_block

    def one_round(round_id, partial_sums):
        block_start = round_id * obs_block

        def take_block(source):
            return lax.dynamic_slice_in_dim(source, block_start, obs_block, 1)

        gram_part, forcing_part = observe(
            anomaly_flat,
            average_flat,
            take_block(cell_ids),
            take_block(class_ids),
            take_block(values),
            take_block(inv_vars),
            take_block(order_ids) < counts[:, None],
            localization_factors,
        )
        return (partial_sums[0] + gram_part, partial_sums[1] + forcing_part)

    initial = (
        jnp.zeros((patches, trial_flattened, trial_flattened), jnp.float32),
        jnp.zeros((patches, trial_flattened), jnp.float32),
    )
    gram_sum, forcing = lax.fori_loop(0, rounds, one_round, initial)
    identity = jnp.eye(trial_flattened, dtype=jnp.float32)
    gram_sum = gram_sum + (trial_flattened - 1) / inflation * identity
    norm_scale = jnp.sqrt(jnp.sum(gram_sum * gram_sum, axis=(1, 2)))
    iterate = gram_sum / norm_scale[:, None, None]
    inverse_root = jnp.broadcast_to(identity, iterate.shape)
    for sweep_id in range(ITERS):
        factor = 1.5 * identity - 0.5 * jnp.einsum(
            "qij,qjk->qik", inverse_root, iterate, precision=lax.Precision.HIGHEST
        )
        if sweep_id + 1 < ITERS:
            iterate = jnp.einsum("qij,qjk->qik", iterate, factor, precision=lax.Precision.HIGHEST)
        inverse_root = jnp.einsum(
            "qij,qjk->qik", factor, inverse_root, precision=lax.Precision.HIGHEST
        )
    partial_shift = jnp.einsum("qij,qj->qi", inverse_root, forcing, precision=lax.Precision.HIGHEST)
    mean_shift = (
        jnp.einsum("qij,qj->qi", inverse_root, partial_shift, precision=lax.Precision.HIGHEST)
        / norm_scale[:, None]
    )
    spread_scale = jnp.sqrt((trial_flattened - 1.0) / norm_scale)
    transform = (spread_scale[:, None, None] * inverse_root + mean_shift[:, :, None]).astype(
        jnp.bfloat16
    )
    own_anomaly = deviation_matrix[
        :, :, REACH_MARGIN : REACH_MARGIN + tile_height, REACH_MARGIN : REACH_MARGIN + tile_width
    ].reshape(trial_flattened, physical_quantity_stack, tile_height, patches, SECTOR_SPAN)
    inner_midpoint = predicted_average[
        :, REACH_MARGIN : REACH_MARGIN + tile_height, REACH_MARGIN : REACH_MARGIN + tile_width
    ].reshape(physical_quantity_stack, tile_height, patches, SECTOR_SPAN)
    analysed = (
        jnp.einsum("kstqp,qkj->jstqp", own_anomaly, transform, preferred_element_type=jnp.float32)
        + inner_midpoint[None]
    )
    analysed = analysed.astype(jnp.bfloat16).reshape(
        trial_flattened, physical_quantity_stack, tile_height, tile_width
    )
    return lax.all_to_all(analysed, "mem", split_axis=0, concat_axis=2, tiled=True)


def solution(mesh):
    placed = (
        P("mem", None, None, "col"),
        P("mem", "col"),
        P("mem", "col", None),
        P("mem", "col", None),
        P("mem", "col", None),
        P("mem", "col", None),
        P(),
    )
    return jax.shard_map(
        local, mesh=mesh, in_specs=placed, out_specs=P("mem", None, None, "col"), check_vma=False
    )
```

profile of v0, /device:TPU:0, one launch (start us, length us, event | category | flops | bytes accessed | tf_op | source)
XLA Modules:
  0.0 388.7 jit_solution(7699056529408383022)
XLA Ops:
  1.9 20.3 %all_to_all.36 = bf16[32,4,32,128]{3,0,1,2:T(8,128)(2,1)S(1)} all-to-all(bf16[32,4,32,128]{3,0,1,2:T(8,128)(2,1)S(1)} %copy.56), channel_id=1, replica_groups=mesh['mem'=8,'col'=4] {'mem'}, dimensions={2} | all-to-all | bytes 2097152 | tf_op jit(solution)/shard_map/all_to_all | solution.py:54
  53.3 7.1 %fusion.29 = f32[1,4,12,136]{3,0,2,1:T(1,128)S(1)} fusion(bf16[256,4,12,4]{3,0,2,1:T(8,128)(2,1)} %copy.62, bf16[256,4,4,128]{3,0,2,1:T(8,128)(2,1)} %copy-done.3, bf16[256,4,4,128]{3,0,2,1:T(8,128)(2,1)} %bitcast.95, bf16[256,4,4,128]{3,0,2,1:T(8,128)(2,1)} %copy-done.2, bf16[256,4,12,4]{3,0,2,1:T(8,128)(2,1)S(1)} %copy.61), kind=kOutput, calls=%fused_computation.60 | convolution fusion | flops 20054016 | bytes 3368448 | tf_op jit(solution)/shard_map/dot_general | solution.py:66
  63.6 8.0 %subtract_convert_fusion = bf16[256,4,12,136]{3,0,2,1:T(8,128)(2,1)S(1)} fusion(f32[4,12,136]{2,1,0:T(8,128)S(1)} %bitcast_multiply_fusion, bf16[256,4,12,4]{3,0,2,1:T(8,128)(2,1)} %copy.62, bf16[256,4,4,128]{3,0,2,1:T(8,128)(2,1)} %copy-done.3, bf16[256,4,4,128]{3,0,2,1:T(8,128)(2,1)} %bitcast.96, bf16[256,4,4,128]{3,0,2,1:T(8,128)(2,1)} %copy-done.2, ...), kind=kLoop, calls=%fused_computation.24 | loop fusion | flops 20054016 | bytes 6710784 | tf_op jit(solution)/shard_map/convert_element_type | solution.py:74
  71.6 5.4 %fusion.33 = (bf16[256,4,12,40]{3,0,2,1:T(8,128)(2,1)}, bf16[256,4,12,40]{3,0,2,1:T(8,128)(2,1)S(1)}, bf16[256,4,12,40]{3,0,2,1:T(8,128)(2,1)}, bf16[256,4,12,40]{3,0,2,1:T(8,128)(2,1)}) fusion(bf16[256,4,12,136]{3,0,2,1:T(8,128)(2,1)S(1)} %subtract_convert_fusion), kind=kLoop, calls=%fused_computation.65 | loop fusion | bytes 7864320 | tf_op jit(solution)/shard_map/slice | solution.py:77
  95.3 234.1 %while.12 = (s32[]{:T(128)}, f32[4,256,256]{2,1,0:T(8,128)S(1)}, f32[4,256]{1,0:T(4,128)S(1)}, s32[]{:T(128)}, s32[4,2048]{1,0:T(4,128)}, /*index=5*/bf16[4,256,...) while((s32[]{:T(128)}, f32[4,256,256]{2,1,0:T(8,128)S(1)}, ...), condition=%wide.region_3.4_spmd, body=%wide.region_1.3_spmd.sunk | while | flops 70158344 | bytes 3735335 | solution.py:121
  102.5 6.6 %gather_fusion.1 = bf16[512,256]{1,0:T(8,128)(2,1)S(1)} fusion(bf16[4,256,1920]{1,2,0:T(8,128)(2,1)} %get-tuple-element.244, s32[512]{0:T(512)S(1)} %fusion.67), kind=kCustom, calls=%fused_computation.clone.1 | custom fusion | bytes 528384 | tf_op jit(solution)/shard_map/while/body/jit(take_along_axis)/gather | solution.py:34
  110.7 4.8 %gather_fusion = f32[512]{0:T(512)S(1)} fusion(f32[4,1920]{1,0:T(4,128)S(1)} %get-tuple-element.251, s32[512]{0:T(512)S(1)} %fusion.67), kind=kCustom, calls=%fused_computation.1.clone.1 | custom fusion | bytes 8192 | tf_op jit(solution)/shard_map/while/body/jit(take_along_axis)/gather | solution.py:35
  117.1 6.6 %gather_fusion.1 = bf16[512,256]{1,0:T(8,128)(2,1)S(1)} fusion(bf16[4,256,1920]{1,2,0:T(8,128)(2,1)} %get-tuple-element.244, s32[512]{0:T(512)S(1)} %fusion.67), kind=kCustom, calls=%fused_computation.clone.1 | custom fusion | bytes 528384 | tf_op jit(solution)/shard_map/while/body/jit(take_along_axis)/gather | solution.py:34
  131.8 6.6 %gather_fusion.1 = bf16[512,256]{1,0:T(8,128)(2,1)S(1)} fusion(bf16[4,256,1920]{1,2,0:T(8,128)(2,1)} %get-tuple-element.244, s32[512]{0:T(512)S(1)} %fusion.67), kind=kCustom, calls=%fused_computation.clone.1 | custom fusion | bytes 528384 | tf_op jit(solution)/shard_map/while/body/jit(take_along_axis)/gather | solution.py:34
  140.0 4.8 %gather_fusion = f32[512]{0:T(512)S(1)} fusion(f32[4,1920]{1,0:T(4,128)S(1)} %get-tuple-element.251, s32[512]{0:T(512)S(1)} %fusion.67), kind=kCustom, calls=%fused_computation.1.clone.1 | custom fusion | bytes 8192 | tf_op jit(solution)/shard_map/while/body/jit(take_along_axis)/gather | solution.py:35
  146.4 6.6 %gather_fusion.1 = bf16[512,256]{1,0:T(8,128)(2,1)S(1)} fusion(bf16[4,256,1920]{1,2,0:T(8,128)(2,1)} %get-tuple-element.244, s32[512]{0:T(512)S(1)} %fusion.67), kind=kCustom, calls=%fused_computation.clone.1 | custom fusion | bytes 528384 | tf_op jit(solution)/shard_map/while/body/jit(take_along_axis)/gather | solution.py:34
  154.6 4.8 %gather_fusion = f32[512]{0:T(512)S(1)} fusion(f32[4,1920]{1,0:T(4,128)S(1)} %get-tuple-element.251, s32[512]{0:T(512)S(1)} %fusion.67), kind=kCustom, calls=%fused_computation.1.clone.1 | custom fusion | bytes 8192 | tf_op jit(solution)/shard_map/while/body/jit(take_along_axis)/gather | solution.py:35
  161.0 6.6 %gather_fusion.1 = bf16[512,256]{1,0:T(8,128)(2,1)S(1)} fusion(bf16[4,256,1920]{1,2,0:T(8,128)(2,1)} %get-tuple-element.244, s32[512]{0:T(512)S(1)} %fusion.67), kind=kCustom, calls=%fused_computation.clone.1 | custom fusion | bytes 528384 | tf_op jit(solution)/shard_map/while/body/jit(take_along_axis)/gather | solution.py:34
  169.2 4.8 %gather_fusion = f32[512]{0:T(512)S(1)} fusion(f32[4,1920]{1,0:T(4,128)S(1)} %get-tuple-element.251, s32[512]{0:T(512)S(1)} %fusion.67), kind=kCustom, calls=%fused_computation.1.clone.1 | custom fusion | bytes 8192 | tf_op jit(solution)/shard_map/while/body/jit(take_along_axis)/gather | solution.py:35
  175.6 6.7 %gather_fusion.1 = bf16[512,256]{1,0:T(8,128)(2,1)S(1)} fusion(bf16[4,256,1920]{1,2,0:T(8,128)(2,1)} %get-tuple-element.244, s32[512]{0:T(512)S(1)} %fusion.67), kind=kCustom, calls=%fused_computation.clone.1 | custom fusion | bytes 528384 | tf_op jit(solution)/shard_map/while/body/jit(take_along_axis)/gather | solution.py:34
  183.9 4.8 %gather_fusion = f32[512]{0:T(512)S(1)} fusion(f32[4,1920]{1,0:T(4,128)S(1)} %get-tuple-element.251, s32[512]{0:T(512)S(1)} %fusion.67), kind=kCustom, calls=%fused_computation.1.clone.1 | custom fusion | bytes 8192 | tf_op jit(solution)/shard_map/while/body/jit(take_along_axis)/gather | solution.py:35
  190.3 6.6 %gather_fusion.1 = bf16[512,256]{1,0:T(8,128)(2,1)S(1)} fusion(bf16[4,256,1920]{1,2,0:T(8,128)(2,1)} %get-tuple-element.244, s32[512]{0:T(512)S(1)} %fusion.67), kind=kCustom, calls=%fused_computation.clone.1 | custom fusion | bytes 528384 | tf_op jit(solution)/shard_map/while/body/jit(take_along_axis)/gather | solution.py:34
  198.5 4.8 %gather_fusion = f32[512]{0:T(512)S(1)} fusion(f32[4,1920]{1,0:T(4,128)S(1)} %get-tuple-element.251, s32[512]{0:T(512)S(1)} %fusion.67), kind=kCustom, calls=%fused_computation.1.clone.1 | custom fusion | bytes 8192 | tf_op jit(solution)/shard_map/while/body/jit(take_along_axis)/gather | solution.py:35
  204.9 6.6 %gather_fusion.1 = bf16[512,256]{1,0:T(8,128)(2,1)S(1)} fusion(bf16[4,256,1920]{1,2,0:T(8,128)(2,1)} %get-tuple-element.244, s32[512]{0:T(512)S(1)} %fusion.67), kind=kCustom, calls=%fused_computation.clone.1 | custom fusion | bytes 528384 | tf_op jit(solution)/shard_map/while/body/jit(take_along_axis)/gather | solution.py:34
  213.1 4.8 %gather_fusion = f32[512]{0:T(512)S(1)} fusion(f32[4,1920]{1,0:T(4,128)S(1)} %get-tuple-element.251, s32[512]{0:T(512)S(1)} %fusion.67), kind=kCustom, calls=%fused_computation.1.clone.1 | custom fusion | bytes 8192 | tf_op jit(solution)/shard_map/while/body/jit(take_along_axis)/gather | solution.py:35
  219.5 6.6 %gather_fusion.1 = bf16[512,256]{1,0:T(8,128)(2,1)S(1)} fusion(bf16[4,256,1920]{1,2,0:T(8,128)(2,1)} %get-tuple-element.244, s32[512]{0:T(512)S(1)} %fusion.67), kind=kCustom, calls=%fused_computation.clone.1 | custom fusion | bytes 528384 | tf_op jit(solution)/shard_map/while/body/jit(take_along_axis)/gather | solution.py:34
  234.1 6.6 %gather_fusion.1 = bf16[512,256]{1,0:T(8,128)(2,1)S(1)} fusion(bf16[4,256,1920]{1,2,0:T(8,128)(2,1)} %get-tuple-element.244, s32[512]{0:T(512)S(1)} %fusion.67), kind=kCustom, calls=%fused_computation.clone.1 | custom fusion | bytes 528384 | tf_op jit(solution)/shard_map/while/body/jit(take_along_axis)/gather | solution.py:34
  248.7 6.6 %gather_fusion.1 = bf16[512,256]{1,0:T(8,128)(2,1)S(1)} fusion(bf16[4,256,1920]{1,2,0:T(8,128)(2,1)} %get-tuple-element.244, s32[512]{0:T(512)S(1)} %fusion.67), kind=kCustom, calls=%fused_computation.clone.1 | custom fusion | bytes 528384 | tf_op jit(solution)/shard_map/while/body/jit(take_along_axis)/gather | solution.py:34
  263.3 6.6 %gather_fusion.1 = bf16[512,256]{1,0:T(8,128)(2,1)S(1)} fusion(bf16[4,256,1920]{1,2,0:T(8,128)(2,1)} %get-tuple-element.244, s32[512]{0:T(512)S(1)} %fusion.67), kind=kCustom, calls=%fused_computation.clone.1 | custom fusion | bytes 528384 | tf_op jit(solution)/shard_map/while/body/jit(take_along_axis)/gather | solution.py:34
  271.5 4.8 %gather_fusion = f32[512]{0:T(512)S(1)} fusion(f32[4,1920]{1,0:T(4,128)S(1)} %get-tuple-element.251, s32[512]{0:T(512)S(1)} %fusion.67), kind=kCustom, calls=%fused_computation.1.clone.1 | custom fusion | bytes 8192 | tf_op jit(solution)/shard_map/while/body/jit(take_along_axis)/gather | solution.py:35
  277.9 6.6 %gather_fusion.1 = bf16[512,256]{1,0:T(8,128)(2,1)S(1)} fusion(bf16[4,256,1920]{1,2,0:T(8,128)(2,1)} %get-tuple-element.244, s32[512]{0:T(512)S(1)} %fusion.67), kind=kCustom, calls=%fused_computation.clone.1 | custom fusion | bytes 528384 | tf_op jit(solution)/shard_map/while/body/jit(take_along_axis)/gather | solution.py:34
  286.1 4.8 %gather_fusion = f32[512]{0:T(512)S(1)} fusion(f32[4,1920]{1,0:T(4,128)S(1)} %get-tuple-element.251, s32[512]{0:T(512)S(1)} %fusion.67), kind=kCustom, calls=%fused_computation.1.clone.1 | custom fusion | bytes 8192 | tf_op jit(solution)/shard_map/while/body/jit(take_along_axis)/gather | solution.py:35
  292.5 6.6 %gather_fusion.1 = bf16[512,256]{1,0:T(8,128)(2,1)S(1)} fusion(bf16[4,256,1920]{1,2,0:T(8,128)(2,1)} %get-tuple-element.244, s32[512]{0:T(512)S(1)} %fusion.67), kind=kCustom, calls=%fused_computation.clone.1 | custom fusion | bytes 528384 | tf_op jit(solution)/shard_map/while/body/jit(take_along_axis)/gather | solution.py:34
  307.2 6.6 %gather_fusion.1 = bf16[512,256]{1,0:T(8,128)(2,1)S(1)} fusion(bf16[4,256,1920]{1,2,0:T(8,128)(2,1)} %get-tuple-element.244, s32[512]{0:T(512)S(1)} %fusion.67), kind=kCustom, calls=%fused_computation.clone.1 | custom fusion | bytes 528384 | tf_op jit(solution)/shard_map/while/body/jit(take_along_axis)/gather | solution.py:34
  315.4 4.8 %gather_fusion = f32[512]{0:T(512)S(1)} fusion(f32[4,1920]{1,0:T(4,128)S(1)} %get-tuple-element.251, s32[512]{0:T(512)S(1)} %fusion.67), kind=kCustom, calls=%fused_computation.1.clone.1 | custom fusion | bytes 8192 | tf_op jit(solution)/shard_map/while/body/jit(take_along_axis)/gather | solution.py:35
  321.8 6.6 %gather_fusion.1 = bf16[512,256]{1,0:T(8,128)(2,1)S(1)} fusion(bf16[4,256,1920]{1,2,0:T(8,128)(2,1)} %get-tuple-element.244, s32[512]{0:T(512)S(1)} %fusion.67), kind=kCustom, calls=%fused_computation.clone.1 | custom fusion | bytes 528384 | tf_op jit(solution)/shard_map/while/body/jit(take_along_axis)/gather | solution.py:34
  349.5 37.4 %all_to_all.37 = bf16[256,4,4,128]{3,2,1,0:T(4,128)(2,1)S(1)} all-to-all(bf16[256,4,4,128]{3,2,1,0:T(4,128)(2,1)S(1)} %copy.71), channel_id=1, replica_groups=mesh['mem'=8,'col'=4] {'mem'}, dimensions={0} | all-to-all | bytes 2097152 | tf_op jit(solution)/shard_map/all_to_all | solution.py:158
  (216 shorter events, 154.4 us)
Async XLA Ops:
  0.0 25.0 %copy-start.7 = (s32[1,4]{1,0:T(1,128)S(1)}, s32[1,4]{1,0:T(1,128)}, u32[]{:S(2)}) copy-start(s32[1,4]{1,0:T(1,128)} %param.10) | copy-start | bytes 52
  22.4 6.7 %copy-start.1 = (bf16[8,32,4,4,128]{4,1,0,3,2:T(8,128)(2,1)}, bf16[8,32,4,4,128]{4,1,0,3,2:T(8,128)(2,1)S(1)}, u32[]{:S(2)}) copy-start(bf16[8,32,4,4,128]{4,1,0,3,2:T(8,128)(2,1)S(1)} %copy.58) | copy-start | bytes 3145732
  22.4 4.7 %collective-permute-start = (bf16[256,4,4,128]{3,0,2,1:T(8,128)(2,1)S(1)}, bf16[256,4,4,128]{3,0,2,1:T(8,128)(2,1)S(1)}, u32[]{:S(2)}, u32[]{:S(2)}) collective-permute-start(bf16[256,4,4,128]{3,0,2,1:T(8,128)(2,1)S(1)} %bitcast.92), channel_id=1, source_target_pairs={{0,4},{4,8},{8,12},{12,16},{16,20},{20,24},{24,28},{1,5},{5,9},{9,... | collective-permute-start | bytes 3145736 | tf_op jit(solution)/shard_map/ppermute | solution.py:18
  23.7 5.3 %collective-permute-start.1 = (bf16[256,4,4,128]{3,0,2,1:T(8,128)(2,1)S(1)}, bf16[256,4,4,128]{3,0,2,1:T(8,128)(2,1)S(1)}, u32[]{:S(2)}, u32[]{:S(2)}) collective-permute-start(bf16[256,4,4,128]{3,0,2,1:T(8,128)(2,1)S(1)} %bitcast.93), channel_id=1, source_target_pairs={{4,0},{8,4},{12,8},{16,12},{20,16},{24,20},{28,24},{5,1},{9,5},{13... | collective-permute-start | bytes 3145736 | tf_op jit(solution)/shard_map/ppermute | solution.py:21
  27.1 1.9 copy-start.2
  29.0 1.0 copy-start.3
  36.6 8.5 %collective-permute-start.2 = (bf16[256,4,12,4]{0,3,2,1:T(4,128)(2,1)S(1)}, bf16[256,4,12,4]{0,3,2,1:T(4,128)(2,1)}, u32[]{:S(2)}, u32[]{:S(2)}) collective-permute-start(bf16[256,4,12,4]{0,3,2,1:T(4,128)(2,1)S(1)} %copy.59), channel_id=1, source_target_pairs={{0,1},{1,2},{2,3},{4,5},{5,6},{6,7},{8,9},{9,10},{10,11},{12,13},{... | collective-permute-start | bytes 294920 | tf_op jit(solution)/shard_map/ppermute | solution.py:18
  42.9 6.8 %collective-permute-start.3 = (bf16[256,4,12,4]{0,3,2,1:T(4,128)(2,1)}, bf16[256,4,12,4]{0,3,2,1:T(4,128)(2,1)}, u32[]{:S(2)}, u32[]{:S(2)}) collective-permute-start(bf16[256,4,12,4]{0,3,2,1:T(4,128)(2,1)} %copy.60), channel_id=1, source_target_pairs={{1,0},{2,1},{3,2},{5,4},{6,5},{7,6},{9,8},{10,9},{11,10},{13,12},{... | collective-permute-start | bytes 294920 | tf_op jit(solution)/shard_map/ppermute | solution.py:21
  71.6 5.4 %copy-start = (bf16[256,4,12,136]{3,0,2,1:T(8,128)(2,1)}, bf16[256,4,12,136]{3,0,2,1:T(8,128)(2,1)S(1)}, u32[]{:S(2)}) copy-start(bf16[256,4,12,136]{3,0,2,1:T(8,128)(2,1)S(1)} %subtract_convert_fusion) | copy-start | bytes 10027012
  85.2 6.3 %copy-start.6 = (f32[1,1920]{1,0:T(1,128)S(1)}, f32[1,1920]{1,0:T(1,128)}, u32[]{:S(2)}) copy-start(f32[1,1920]{1,0:T(1,128)} %stack.37) | copy-start | bytes 23044
  91.5 3.8 copy-start.8
  91.5 3.8 copy-start.9
  95.3 234.2 %copy-start.4 = (f32[256,256]{1,0:T(8,128)S(1)}, f32[256,256]{1,0:T(8,128)}, u32[]{:S(2)}) copy-start(f32[256,256]{1,0:T(8,128)} %get-tuple-element.118) | copy-start | bytes 786436
  95.3 234.4 %copy-start.5 = (f32[256,256]{1,0:T(8,128)S(1)}, f32[256,256]{1,0:T(8,128)}, u32[]{:S(2)}) copy-start(f32[256,256]{1,0:T(8,128)} %fusion.22) | copy-start | bytes 786436
where the time goes:
time: 392 us; the launch traced here: 389 us
  local copies, waits for them, and re-layouts  243 us (62%)
  blocking collectives  57.8 us (15%)
  other arithmetic  39.9 us (10%)
  matrix products  33.8 us (9%)
  starting transfers between devices  8.24 us (2%)
  waiting for transfers between devices  3.97 us (1%)
    gather x32, local copies, waits for them, and re-layouts, observe(): observed = jnp.take_along_axis(anomaly_flat, cell_ids[:, None, :], axis=2)  108 us
    gather x16, local copies, waits for them, and re-layouts, observe(): innovation = values - jnp.take_along_axis(average_flat, cell_ids, axis=1)  77.3 us
    all_to_all x1, blocking collectives, local(): lax.all_to_all(analysed, 'mem', split_axis=0, concat_axis=2, tiled=True)  37.4 us
    all_to_all x1, blocking collectives, local(): lax.all_to_all(background_trials, 'mem', split_axis=2, concat_axis=0, til...  20.3 us
    slice x5, local copies, waits for them, and re-layouts, local(): deviation_matrix[:, :, :, sector_index * SECTOR_SPAN:sector_index * SECTO...  19.8 us
    sub x16, other arithmetic, observe(): innovation = values - jnp.take_along_axis(average_flat, cell_ids, axis=1)  12.5 us
    gather x16, other arithmetic, observe(): observed = jnp.take_along_axis(anomaly_flat, cell_ids[:, None, :], axis=2)  11.2 us
    dynamic_slice x16, local copies, waits for them, and re-layouts, take_block(): return lax.dynamic_slice_in_dim(source, block_start, obs_block, 1)  11 us
  transfers between devices with their start and end apart: 4, of which 2 were waited for; matrix products, arithmetic and copies ran while one was open for 2% of the time, Pallas kernels for 0%

commit v1 on v0

--- a/solution.py
+++ b/solution.py
@@ -8,6 +8,12 @@
 ITERS = 4
 inflation = 1.1
 obs_block = 128
+
+
+def trade_parts(x, name, split, join):
+    cells = jnp.split(x, lax.axis_size(name), axis=split)
+    got = lax.all_to_all(jnp.stack(cells), name, 0, 0)
+    return jnp.concatenate(got, axis=join)
 
 
 def padded(block, sides, width):
@@ -155,7 +161,7 @@
     analysed = analysed.astype(jnp.bfloat16).reshape(
         trial_flattened, physical_quantity_stack, tile_height, tile_width
     )
-    return lax.all_to_all(analysed, "mem", split_axis=0, concat_axis=2, tiled=True)
+    return trade_parts(analysed, "mem", 0, 2)
 
 
 def solution(mesh):

time: 392 us -> 411 us (1.048)
  local copies, waits for them, and re-layouts: 243 us -> 258 us
    split x0 -> x9, local copies, waits for them, and re-layouts: none -> 8.96 us  [trade_parts(): cells = jnp.split(x, lax.axis_size(name), axis=split)]
    another operation x0 -> x9, local copies, waits for them, and re-layouts: none -> 6.89 us  [trade_parts(): got = lax.all_to_all(jnp.stack(cells), name, 0, 0)]
where the time goes in v1:
time: 411 us; the launch traced here: 404 us
  local copies, waits for them, and re-layouts  258 us (63%)
  blocking collectives  57.6 us (14%)
  other arithmetic  39.9 us (10%)
  matrix products  33.7 us (8%)
  starting transfers between devices  8.52 us (2%)
    gather x32, local copies, waits for them, and re-layouts, observe(): observed = jnp.take_along_axis(anomaly_flat, cell_ids[:, None, :], axis=2)  109 us
    gather x16, local copies, waits for them, and re-layouts, observe(): innovation = values - jnp.take_along_axis(average_flat, cell_ids, axis=1)  77.3 us
    all_to_all x1, blocking collectives, trade_parts(): got = lax.all_to_all(jnp.stack(cells), name, 0, 0)  37.3 us
    all_to_all x1, blocking collectives, local(): lax.all_to_all(background_trials, 'mem', split_axis=2, concat_axis=0, til...  20.3 us
    slice x5, local copies, waits for them, and re-layouts, local(): deviation_matrix[:, :, :, sector_index * SECTOR_SPAN:sector_index * SECTO...  19.9 us
    sub x16, other arithmetic, observe(): innovation = values - jnp.take_along_axis(average_flat, cell_ids, axis=1)  12.5 us
    gather x16, other arithmetic, observe(): observed = jnp.take_along_axis(anomaly_flat, cell_ids[:, None, :], axis=2)  11.2 us
    dynamic_slice x16, local copies, waits for them, and re-layouts, take_block(): return lax.dynamic_slice_in_dim(source, block_start, obs_block, 1)  11 us
  transfers between devices with their start and end apart: 4, of which 2 were waited for; matrix products, arithmetic and copies ran while one was open for 2% of the time, Pallas kernels for 0%

profile of v1, /device:TPU:0, one launch (start us, length us, event | category | flops | bytes accessed | tf_op | source)
XLA Modules:
  0.0 404.2 jit_solution(6175401384580795290)
XLA Ops:
  1.9 20.3 %all_to_all.23 = bf16[32,4,32,128]{3,0,1,2:T(8,128)(2,1)S(1)} all-to-all(bf16[32,4,32,128]{3,0,1,2:T(8,128)(2,1)S(1)} %copy.73), channel_id=1, replica_groups=mesh['mem'=8,'col'=4] {'mem'}, dimensions={2} | all-to-all | bytes 2097152 | tf_op jit(solution)/shard_map/all_to_all | solution.py:60
  53.3 7.1 %fusion.29 = f32[1,4,12,136]{3,0,2,1:T(1,128)S(1)} fusion(bf16[256,4,12,4]{3,0,2,1:T(8,128)(2,1)} %copy.79, bf16[256,4,4,128]{3,0,2,1:T(8,128)(2,1)} %copy-done.3, bf16[256,4,4,128]{3,0,2,1:T(8,128)(2,1)} %bitcast.108, bf16[256,4,4,128]{3,0,2,1:T(8,128)(2,1)} %copy-done.2, bf16[256,4,12,4]{3,0,2,1:T(8,128)(2,1)S(1)} %copy.78), kind=kOutput, calls=%fused_computation.68 | convolution fusion | flops 20054016 | bytes 3368448 | tf_op jit(solution)/shard_map/dot_general | solution.py:72
  63.6 8.0 %subtract_convert_fusion = bf16[256,4,12,136]{3,0,2,1:T(8,128)(2,1)S(1)} fusion(f32[4,12,136]{2,1,0:T(8,128)S(1)} %bitcast_multiply_fusion, bf16[256,4,12,4]{3,0,2,1:T(8,128)(2,1)} %copy.79, bf16[256,4,4,128]{3,0,2,1:T(8,128)(2,1)} %copy-done.3, bf16[256,4,4,128]{3,0,2,1:T(8,128)(2,1)} %bitcast.109, bf16[256,4,4,128]{3,0,2,1:T(8,128)(2,1)} %copy-done.2, ...), kind=kLoop, calls=%fused_computation.24 | loop fusion | flops 20054016 | bytes 6710784 | tf_op jit(solution)/shard_map/convert_element_type | solution.py:80
  71.6 5.4 %fusion.33 = (bf16[256,4,12,40]{3,0,2,1:T(8,128)(2,1)}, bf16[256,4,12,40]{3,0,2,1:T(8,128)(2,1)S(1)}, bf16[256,4,12,40]{3,0,2,1:T(8,128)(2,1)}, bf16[256,4,12,40]{3,0,2,1:T(8,128)(2,1)}) fusion(bf16[256,4,12,136]{3,0,2,1:T(8,128)(2,1)S(1)} %subtract_convert_fusion), kind=kLoop, calls=%fused_computation.73 | loop fusion | bytes 7864320 | tf_op jit(solution)/shard_map/slice | solution.py:83
  95.4 234.3 %while.12 = (s32[]{:T(128)}, f32[4,256,256]{2,1,0:T(8,128)S(1)}, f32[4,256]{1,0:T(4,128)S(1)}, s32[]{:T(128)}, s32[4,2048]{1,0:T(4,128)}, /*index=5*/bf16[4,256,...) while((s32[]{:T(128)}, f32[4,256,256]{2,1,0:T(8,128)S(1)}, ...), condition=%wide.region_3.4_spmd, body=%wide.region_1.3_spmd.sunk | while | flops 70158344 | bytes 3735335 | solution.py:127
  96.2 4.8 %gather_fusion = f32[512]{0:T(512)S(1)} fusion(f32[4,1920]{1,0:T(4,128)S(1)} %get-tuple-element.259, s32[512]{0:T(512)S(1)} %fusion.68), kind=kCustom, calls=%fused_computation.1.clone.1 | custom fusion | bytes 8192 | tf_op jit(solution)/shard_map/while/body/jit(take_along_axis)/gather | solution.py:41
  102.6 6.6 %gather_fusion.1 = bf16[512,256]{1,0:T(8,128)(2,1)S(1)} fusion(bf16[4,256,1920]{1,2,0:T(8,128)(2,1)} %get-tuple-element.252, s32[512]{0:T(512)S(1)} %fusion.68), kind=kCustom, calls=%fused_computation.clone.1 | custom fusion | bytes 528384 | tf_op jit(solution)/shard_map/while/body/jit(take_along_axis)/gather | solution.py:40
  110.8 4.8 %gather_fusion = f32[512]{0:T(512)S(1)} fusion(f32[4,1920]{1,0:T(4,128)S(1)} %get-tuple-element.259, s32[512]{0:T(512)S(1)} %fusion.68), kind=kCustom, calls=%fused_computation.1.clone.1 | custom fusion | bytes 8192 | tf_op jit(solution)/shard_map/while/body/jit(take_along_axis)/gather | solution.py:41
  117.2 6.6 %gather_fusion.1 = bf16[512,256]{1,0:T(8,128)(2,1)S(1)} fusion(bf16[4,256,1920]{1,2,0:T(8,128)(2,1)} %get-tuple-element.252, s32[512]{0:T(512)S(1)} %fusion.68), kind=kCustom, calls=%fused_computation.clone.1 | custom fusion | bytes 528384 | tf_op jit(solution)/shard_map/while/body/jit(take_along_axis)/gather | solution.py:40
  125.4 4.8 %gather_fusion = f32[512]{0:T(512)S(1)} fusion(f32[4,1920]{1,0:T(4,128)S(1)} %get-tuple-element.259, s32[512]{0:T(512)S(1)} %fusion.68), kind=kCustom, calls=%fused_computation.1.clone.1 | custom fusion | bytes 8192 | tf_op jit(solution)/shard_map/while/body/jit(take_along_axis)/gather | solution.py:41
  131.8 6.7 %gather_fusion.1 = bf16[512,256]{1,0:T(8,128)(2,1)S(1)} fusion(bf16[4,256,1920]{1,2,0:T(8,128)(2,1)} %get-tuple-element.252, s32[512]{0:T(512)S(1)} %fusion.68), kind=kCustom, calls=%fused_computation.clone.1 | custom fusion | bytes 528384 | tf_op jit(solution)/shard_map/while/body/jit(take_along_axis)/gather | solution.py:40
  140.1 4.8 %gather_fusion = f32[512]{0:T(512)S(1)} fusion(f32[4,1920]{1,0:T(4,128)S(1)} %get-tuple-element.259, s32[512]{0:T(512)S(1)} %fusion.68), kind=kCustom, calls=%fused_computation.1.clone.1 | custom fusion | bytes 8192 | tf_op jit(solution)/shard_map/while/body/jit(take_along_axis)/gather | solution.py:41
  146.5 6.6 %gather_fusion.1 = bf16[512,256]{1,0:T(8,128)(2,1)S(1)} fusion(bf16[4,256,1920]{1,2,0:T(8,128)(2,1)} %get-tuple-element.252, s32[512]{0:T(512)S(1)} %fusion.68), kind=kCustom, calls=%fused_computation.clone.1 | custom fusion | bytes 528384 | tf_op jit(solution)/shard_map/while/body/jit(take_along_axis)/gather | solution.py:40
  161.1 6.6 %gather_fusion.1 = bf16[512,256]{1,0:T(8,128)(2,1)S(1)} fusion(bf16[4,256,1920]{1,2,0:T(8,128)(2,1)} %get-tuple-element.252, s32[512]{0:T(512)S(1)} %fusion.68), kind=kCustom, calls=%fused_computation.clone.1 | custom fusion | bytes 528384 | tf_op jit(solution)/shard_map/while/body/jit(take_along_axis)/gather | solution.py:40
  175.7 6.6 %gather_fusion.1 = bf16[512,256]{1,0:T(8,128)(2,1)S(1)} fusion(bf16[4,256,1920]{1,2,0:T(8,128)(2,1)} %get-tuple-element.252, s32[512]{0:T(512)S(1)} %fusion.68), kind=kCustom, calls=%fused_computation.clone.1 | custom fusion | bytes 528384 | tf_op jit(solution)/shard_map/while/body/jit(take_along_axis)/gather | solution.py:40
  184.0 4.8 %gather_fusion = f32[512]{0:T(512)S(1)} fusion(f32[4,1920]{1,0:T(4,128)S(1)} %get-tuple-element.259, s32[512]{0:T(512)S(1)} %fusion.68), kind=kCustom, calls=%fused_computation.1.clone.1 | custom fusion | bytes 8192 | tf_op jit(solution)/shard_map/while/body/jit(take_along_axis)/gather | solution.py:41
  190.4 6.6 %gather_fusion.1 = bf16[512,256]{1,0:T(8,128)(2,1)S(1)} fusion(bf16[4,256,1920]{1,2,0:T(8,128)(2,1)} %get-tuple-element.252, s32[512]{0:T(512)S(1)} %fusion.68), kind=kCustom, calls=%fused_computation.clone.1 | custom fusion | bytes 528384 | tf_op jit(solution)/shard_map/while/body/jit(take_along_axis)/gather | solution.py:40
  198.6 4.8 %gather_fusion = f32[512]{0:T(512)S(1)} fusion(f32[4,1920]{1,0:T(4,128)S(1)} %get-tuple-element.259, s32[512]{0:T(512)S(1)} %fusion.68), kind=kCustom, calls=%fused_computation.1.clone.1 | custom fusion | bytes 8192 | tf_op jit(solution)/shard_map/while/body/jit(take_along_axis)/gather | solution.py:41
  205.0 6.6 %gather_fusion.1 = bf16[512,256]{1,0:T(8,128)(2,1)S(1)} fusion(bf16[4,256,1920]{1,2,0:T(8,128)(2,1)} %get-tuple-element.252, s32[512]{0:T(512)S(1)} %fusion.68), kind=kCustom, calls=%fused_computation.clone.1 | custom fusion | bytes 528384 | tf_op jit(solution)/shard_map/while/body/jit(take_along_axis)/gather | solution.py:40
  219.6 6.6 %gather_fusion.1 = bf16[512,256]{1,0:T(8,128)(2,1)S(1)} fusion(bf16[4,256,1920]{1,2,0:T(8,128)(2,1)} %get-tuple-element.252, s32[512]{0:T(512)S(1)} %fusion.68), kind=kCustom, calls=%fused_computation.clone.1 | custom fusion | bytes 528384 | tf_op jit(solution)/shard_map/while/body/jit(take_along_axis)/gather | solution.py:40
  234.2 6.6 %gather_fusion.1 = bf16[512,256]{1,0:T(8,128)(2,1)S(1)} fusion(bf16[4,256,1920]{1,2,0:T(8,128)(2,1)} %get-tuple-element.252, s32[512]{0:T(512)S(1)} %fusion.68), kind=kCustom, calls=%fused_computation.clone.1 | custom fusion | bytes 528384 | tf_op jit(solution)/shard_map/while/body/jit(take_along_axis)/gather | solution.py:40
  242.5 4.8 %gather_fusion = f32[512]{0:T(512)S(1)} fusion(f32[4,1920]{1,0:T(4,128)S(1)} %get-tuple-element.259, s32[512]{0:T(512)S(1)} %fusion.68), kind=kCustom, calls=%fused_computation.1.clone.1 | custom fusion | bytes 8192 | tf_op jit(solution)/shard_map/while/body/jit(take_along_axis)/gather | solution.py:41
  248.9 6.6 %gather_fusion.1 = bf16[512,256]{1,0:T(8,128)(2,1)S(1)} fusion(bf16[4,256,1920]{1,2,0:T(8,128)(2,1)} %get-tuple-element.252, s32[512]{0:T(512)S(1)} %fusion.68), kind=kCustom, calls=%fused_computation.clone.1 | custom fusion | bytes 528384 | tf_op jit(solution)/shard_map/while/body/jit(take_along_axis)/gather | solution.py:40
  257.1 4.8 %gather_fusion = f32[512]{0:T(512)S(1)} fusion(f32[4,1920]{1,0:T(4,128)S(1)} %get-tuple-element.259, s32[512]{0:T(512)S(1)} %fusion.68), kind=kCustom, calls=%fused_computation.1.clone.1 | custom fusion | bytes 8192 | tf_op jit(solution)/shard_map/while/body/jit(take_along_axis)/gather | solution.py:41
  263.5 6.6 %gather_fusion.1 = bf16[512,256]{1,0:T(8,128)(2,1)S(1)} fusion(bf16[4,256,1920]{1,2,0:T(8,128)(2,1)} %get-tuple-element.252, s32[512]{0:T(512)S(1)} %fusion.68), kind=kCustom, calls=%fused_computation.clone.1 | custom fusion | bytes 528384 | tf_op jit(solution)/shard_map/while/body/jit(take_along_axis)/gather | solution.py:40
  278.1 6.6 %gather_fusion.1 = bf16[512,256]{1,0:T(8,128)(2,1)S(1)} fusion(bf16[4,256,1920]{1,2,0:T(8,128)(2,1)} %get-tuple-element.252, s32[512]{0:T(512)S(1)} %fusion.68), kind=kCustom, calls=%fused_computation.clone.1 | custom fusion | bytes 528384 | tf_op jit(solution)/shard_map/while/body/jit(take_along_axis)/gather | solution.py:40
  286.3 4.8 %gather_fusion = f32[512]{0:T(512)S(1)} fusion(f32[4,1920]{1,0:T(4,128)S(1)} %get-tuple-element.259, s32[512]{0:T(512)S(1)} %fusion.68), kind=kCustom, calls=%fused_computation.1.clone.1 | custom fusion | bytes 8192 | tf_op jit(solution)/shard_map/while/body/jit(take_along_axis)/gather | solution.py:41
  292.7 6.6 %gather_fusion.1 = bf16[512,256]{1,0:T(8,128)(2,1)S(1)} fusion(bf16[4,256,1920]{1,2,0:T(8,128)(2,1)} %get-tuple-element.252, s32[512]{0:T(512)S(1)} %fusion.68), kind=kCustom, calls=%fused_computation.clone.1 | custom fusion | bytes 528384 | tf_op jit(solution)/shard_map/while/body/jit(take_along_axis)/gather | solution.py:40
  307.4 6.6 %gather_fusion.1 = bf16[512,256]{1,0:T(8,128)(2,1)S(1)} fusion(bf16[4,256,1920]{1,2,0:T(8,128)(2,1)} %get-tuple-element.252, s32[512]{0:T(512)S(1)} %fusion.68), kind=kCustom, calls=%fused_computation.clone.1 | custom fusion | bytes 528384 | tf_op jit(solution)/shard_map/while/body/jit(take_along_axis)/gather | solution.py:40
  315.6 4.8 %gather_fusion = f32[512]{0:T(512)S(1)} fusion(f32[4,1920]{1,0:T(4,128)S(1)} %get-tuple-element.259, s32[512]{0:T(512)S(1)} %fusion.68), kind=kCustom, calls=%fused_computation.1.clone.1 | custom fusion | bytes 8192 | tf_op jit(solution)/shard_map/while/body/jit(take_along_axis)/gather | solution.py:41
  322.0 6.6 %gather_fusion.1 = bf16[512,256]{1,0:T(8,128)(2,1)S(1)} fusion(bf16[4,256,1920]{1,2,0:T(8,128)(2,1)} %get-tuple-element.252, s32[512]{0:T(512)S(1)} %fusion.68), kind=kCustom, calls=%fused_computation.clone.1 | custom fusion | bytes 528384 | tf_op jit(solution)/shard_map/while/body/jit(take_along_axis)/gather | solution.py:40
  365.2 37.3 %all_to_all.24 = bf16[8,32,4,4,128]{4,1,3,2,0:T(8,128)(2,1)S(1)} all-to-all(bf16[8,32,4,4,128]{4,1,3,2,0:T(8,128)(2,1)S(1)} %constant_dynamic-update-slice_fusion), channel_id=1, replica_groups=mesh['mem'=8,'col'=4] {'mem'}, dimensions={0} | all-to-all | bytes 2097152 | tf_op jit(solution)/shard_map/all_to_all | solution.py:15
  (244 shorter events, 169.6 us)
Async XLA Ops:
  0.0 25.0 %copy-start.10 = (s32[1,4]{1,0:T(1,128)S(1)}, s32[1,4]{1,0:T(1,128)}, u32[]{:S(2)}) copy-start(s32[1,4]{1,0:T(1,128)} %param.10) | copy-start | bytes 52
  22.4 6.7 %copy-start.1 = (bf16[8,32,4,4,128]{4,1,0,3,2:T(8,128)(2,1)}, bf16[8,32,4,4,128]{4,1,0,3,2:T(8,128)(2,1)S(1)}, u32[]{:S(2)}) copy-start(bf16[8,32,4,4,128]{4,1,0,3,2:T(8,128)(2,1)S(1)} %copy.75) | copy-start | bytes 3145732
  22.4 4.7 %collective-permute-start = (bf16[256,4,4,128]{3,0,2,1:T(8,128)(2,1)S(1)}, bf16[256,4,4,128]{3,0,2,1:T(8,128)(2,1)S(1)}, u32[]{:S(2)}, u32[]{:S(2)}) collective-permute-start(bf16[256,4,4,128]{3,0,2,1:T(8,128)(2,1)S(1)} %bitcast.105), channel_id=1, source_target_pairs={{0,4},{4,8},{8,12},{12,16},{16,20},{20,24},{24,28},{1,5},{5,9},{9,... | collective-permute-start | bytes 3145736 | tf_op jit(solution)/shard_map/ppermute | solution.py:24
  23.7 5.3 %collective-permute-start.1 = (bf16[256,4,4,128]{3,0,2,1:T(8,128)(2,1)S(1)}, bf16[256,4,4,128]{3,0,2,1:T(8,128)(2,1)S(1)}, u32[]{:S(2)}, u32[]{:S(2)}) collective-permute-start(bf16[256,4,4,128]{3,0,2,1:T(8,128)(2,1)S(1)} %bitcast.106), channel_id=1, source_target_pairs={{4,0},{8,4},{12,8},{16,12},{20,16},{24,20},{28,24},{5,1},{9,5},{13... | collective-permute-start | bytes 3145736 | tf_op jit(solution)/shard_map/ppermute | solution.py:27
  27.1 1.9 copy-start.2
  29.0 1.0 copy-start.3
  36.7 8.7 %collective-permute-start.2 = (bf16[256,4,12,4]{0,3,2,1:T(4,128)(2,1)S(1)}, bf16[256,4,12,4]{0,3,2,1:T(4,128)(2,1)}, u32[]{:S(2)}, u32[]{:S(2)}) collective-permute-start(bf16[256,4,12,4]{0,3,2,1:T(4,128)(2,1)S(1)} %copy.76), channel_id=1, source_target_pairs={{0,1},{1,2},{2,3},{4,5},{5,6},{6,7},{8,9},{9,10},{10,11},{12,13},{... | collective-permute-start | bytes 294920 | tf_op jit(solution)/shard_map/ppermute | solution.py:24
  42.9 6.8 %collective-permute-start.3 = (bf16[256,4,12,4]{0,3,2,1:T(4,128)(2,1)}, bf16[256,4,12,4]{0,3,2,1:T(4,128)(2,1)}, u32[]{:S(2)}, u32[]{:S(2)}) collective-permute-start(bf16[256,4,12,4]{0,3,2,1:T(4,128)(2,1)} %copy.77), channel_id=1, source_target_pairs={{1,0},{2,1},{3,2},{5,4},{6,5},{7,6},{9,8},{10,9},{11,10},{13,12},{... | collective-permute-start | bytes 294920 | tf_op jit(solution)/shard_map/ppermute | solution.py:27
  71.6 5.4 %copy-start = (bf16[256,4,12,136]{3,0,2,1:T(8,128)(2,1)}, bf16[256,4,12,136]{3,0,2,1:T(8,128)(2,1)S(1)}, u32[]{:S(2)}) copy-start(bf16[256,4,12,136]{3,0,2,1:T(8,128)(2,1)S(1)} %subtract_convert_fusion) | copy-start | bytes 10027012
  85.2 6.3 %copy-start.9 = (f32[1,1920]{1,0:T(1,128)S(1)}, f32[1,1920]{1,0:T(1,128)}, u32[]{:S(2)}) copy-start(f32[1,1920]{1,0:T(1,128)} %stack.64) | copy-start | bytes 23044
  91.6 3.8 copy-start.11
  91.6 3.8 copy-start.12
  95.4 234.3 %copy-start.5 = (f32[256,256]{1,0:T(8,128)S(1)}, f32[256,256]{1,0:T(8,128)}, u32[]{:S(2)}) copy-start(f32[256,256]{1,0:T(8,128)} %get-tuple-element.126) | copy-start | bytes 786436
  95.4 234.5 %copy-start.6 = (f32[256,256]{1,0:T(8,128)S(1)}, f32[256,256]{1,0:T(8,128)}, u32[]{:S(2)}) copy-start(f32[256,256]{1,0:T(8,128)} %fusion.22) | copy-start | bytes 786436
  362.6 2.5 copy-start.4
  363.8 1.3 copy-start.7
  363.8 1.3 copy-start.8
